TPU v7x, 512 devices: a whole 4x4x16 slice. The times are simulated.
512 devices in a mesh: space: 128 (over y, z, core), level: 4 (over x).
Axes of the slice: x: 4, y: 4, z: 16, core: 2. Of those that a mesh axis runs over, the one named last changes fastest.
Arguments:
- grid_latent: bfloat16 [65536, 512], P('space'), may hold values from -6 to 6
- mesh_latent: bfloat16 [4, 1024, 512], P('level', 'space'), may hold values from -6 to 6
- grid_output_cotangent: bfloat16 [65536, 512], P('space'), may hold values from -6 to 6
- w_send: bfloat16 [512, 512], replicated, may hold values from -0.25 to 0.25
- w_recv: bfloat16 [512, 512], replicated, may hold values from -0.25 to 0.25
- output_weight: bfloat16 [512, 512], replicated, may hold values from -0.25 to 0.25
- hidden_layer_bias: float32 [512], replicated, may hold values from -4 to 4
- output_norm_gain: float32 [512], replicated, may hold values from 0.1 to 1.9
- edge_sender: int32 [4, 262144], P('level', 'space'), may hold values from 0 to 23
- edge_receiver: int32 [4, 262144], P('level', 'space'), may hold values from 0 to 511
- edge_live: int32 [4, 262144], P('level', 'space'), may hold values 0 or 1
Outputs:
- d_grid: float32 [65536, 512], P(('space', 'level'))
- d_mesh: float32 [4, 1024, 512], P('level', 'space')
- d_w_send: bfloat16 [512, 512], replicated
- d_w_recv: bfloat16 [512, 512], replicated
- d_w_out: bfloat16 [512, 512], replicated
- d_bias: float32 [512], replicated
- d_gain: float32 [512], replicated
All inputs are finite; a program needn't handle non-finite values. No bound on the sum of `edge_live` on one device may be relied on, other than what follows from the above.
Results may differ from a plain program's by a relative error of at most 0.012.
Values may be sent and summed in bfloat16 or wider, within the bound.
A program may use at most 64 MiB of HBM per device.

v0:
```python
import jax
import jax.numpy as jnp
from jax import lax
from jax.sharding import PartitionSpec as P


def with_halo(cells, sides, width):
    for axis, dim in sides:
        count = lax.axis_size(axis)
        ends = count - 1
        head = lax.slice_in_dim(cells, 0, width, axis=dim)
        tail = lax.slice_in_dim(cells, cells.shape[dim] - width, cells.shape[dim], axis=dim)
        cells = jnp.concatenate(
            [
                lax.ppermute(tail, axis, [(i, (i + 1) % count) for i in range(ends)]),
                cells,
                lax.ppermute(head, axis, [((i + 1) % count, i) for i in range(ends)]),
            ],
            axis=dim,
        )
    return cells


def from_behind(block, axis, distance):
    devices = range(lax.axis_size(axis))
    route = [(i - distance, i) for i in devices if i - distance in devices]
    return lax.ppermute(block, axis, route)


def in_blocks(value, dim, peers):
    before, after = (value.shape[:dim], value.shape[dim + 1 :])
    return jnp.moveaxis(value.reshape(*before, peers, -1, *after), dim, 0)


def summed_on_arrival(value, axis, dim):
    peers = lax.axis_size(axis)
    tiles = lax.all_to_all(in_blocks(value, dim, peers), axis, 0, 0, tiled=True)
    return jnp.sum(tiles.astype(jnp.float32), axis=0)


def edge_reverse_step(
    sending_rows,
    receiver_rows,
    cotangent_lines,
    slot_active_flags,
    output_weight,
    hidden_layer_bias,
    output_norm_gain,
):
    preact = sending_rows + receiver_rows + hidden_layer_bias
    hidden = jax.nn.silu(preact).astype(jnp.bfloat16)
    outer = jnp.dot(hidden, output_weight, preferred_element_type=jnp.float32)
    center = outer - jnp.mean(outer, axis=-1, keepdims=True)
    inv_scale = lax.rsqrt(jnp.mean(center * center, axis=-1, keepdims=True) + 1e-05)
    normed = center * inv_scale
    incoming_gradient = cotangent_lines.astype(jnp.float32) * slot_active_flags[:, None].astype(
        jnp.float32
    )
    scaled = incoming_gradient * output_norm_gain
    d_outer = inv_scale * (
        scaled
        - jnp.mean(scaled, axis=-1, keepdims=True)
        - normed * jnp.mean(scaled * normed, axis=-1, keepdims=True)
    )
    d_outer_b = d_outer.astype(jnp.bfloat16)
    w_out_grad = jnp.dot(hidden.T, d_outer_b, preferred_element_type=jnp.float32)
    d_hidden = jnp.dot(d_outer_b, output_weight.T, preferred_element_type=jnp.float32)
    sigmoid = jax.nn.sigmoid(preact)
    preactivation_gradient = d_hidden * sigmoid * (1.0 + preact * (1.0 - sigmoid))
    return (
        preactivation_gradient,
        w_out_grad,
        jnp.sum(preactivation_gradient, axis=0),
        jnp.sum(incoming_gradient * normed, axis=0),
    )


def body(
    grid_latent,
    mesh_latent,
    grid_output_cotangent,
    w_send,
    w_recv,
    output_weight,
    hidden_layer_bias,
    output_norm_gain,
    edge_sender,
    edge_receiver,
    edge_live,
):
    shards = lax.axis_size("space")
    width = grid_latent.shape[1]
    grid_rows = grid_latent.shape[0]
    mesh_rows = mesh_latent.shape[1]
    slots = edge_sender.shape[1]
    sender_local = edge_sender[0]
    receiver_index = edge_receiver[0]
    band = lax.axis_index("space")
    window = sender_local // mesh_rows
    target = band + window - 1
    inside = (target >= 0) & (target < shards)
    window = jnp.where(inside, window, 1)
    table_row = window * mesh_rows + sender_local % mesh_rows
    proj_send = jnp.dot(mesh_latent[0], w_send, preferred_element_type=jnp.float32).astype(
        jnp.bfloat16
    )
    projected_receiver = jnp.dot(grid_latent, w_recv, preferred_element_type=jnp.float32)
    table = with_halo(proj_send, (("space", 0),), mesh_rows)
    sending_rows = table[table_row]
    block = 512
    blocks = slots // block

    def run_block(operands):
        rows_send, rows_recv, rows_cot, rows_live = operands
        return edge_reverse_step(
            rows_send.astype(jnp.float32),
            rows_recv,
            rows_cot,
            rows_live,
            output_weight,
            hidden_layer_bias,
            output_norm_gain,
        )

    operands = (
        sending_rows.reshape(blocks, block, width),
        projected_receiver[receiver_index].reshape(blocks, block, width),
        grid_output_cotangent[receiver_index].reshape(blocks, block, width),
        edge_live[0].reshape(blocks, block),
    )
    d_pre_blocks, wout_blocks, bias_blocks, gain_blocks = lax.map(run_block, operands)
    preactivation_gradient = d_pre_blocks.reshape(slots, width)
    output_weight_piece = jnp.sum(wout_blocks, axis=0)
    bias_piece = jnp.sum(bias_blocks, axis=0)
    gain_piece = jnp.sum(gain_blocks, axis=0)
    table_grads = jax.ops.segment_sum(preactivation_gradient, table_row, num_segments=3 * mesh_rows)
    below = table_grads[:mesh_rows]
    above = table_grads[2 * mesh_rows :]
    from_below = from_behind(above, "space", 1)
    from_above = from_behind(below, "space", -1)
    mesh_acc = table_grads[mesh_rows : 2 * mesh_rows] + from_below + from_above
    grid_local = jax.ops.segment_sum(preactivation_gradient, receiver_index, num_segments=grid_rows)
    share = grid_rows // lax.axis_size("level")
    offset = lax.axis_index("level") * share
    grid_acc = summed_on_arrival(grid_local.astype(jnp.bfloat16), "level", 0)
    grid_part = lax.dynamic_slice_in_dim(grid_latent, offset, share, 0)
    mesh_sum = mesh_acc.astype(jnp.bfloat16)
    grid_sum = grid_acc.astype(jnp.bfloat16)
    d_mesh = jnp.dot(mesh_sum, w_send.T, preferred_element_type=jnp.float32)[None]
    d_grid = jnp.dot(grid_sum, w_recv.T, preferred_element_type=jnp.float32)
    wsend_part = jnp.dot(mesh_latent[0].T, mesh_sum, preferred_element_type=jnp.float32)
    wrecv_part = jnp.dot(grid_part.T, grid_sum, preferred_element_type=jnp.float32)
    totals = lax.psum(
        (wsend_part, wrecv_part, output_weight_piece, bias_piece, gain_piece), ("space", "level")
    )
    d_w_send = totals[0].astype(jnp.bfloat16)
    d_w_recv = totals[1].astype(jnp.bfloat16)
    d_w_out = totals[2].astype(jnp.bfloat16)
    d_bias = totals[3]
    d_gain = totals[4]
    return (d_grid, d_mesh, d_w_send, d_w_recv, d_w_out, d_bias, d_gain)


def solution(mesh):
    return jax.shard_map(
        body,
        mesh=mesh,
        in_specs=(
            P("space", None),
            P("level", "space", None),
            P("space", None),
            P(),
            P(),
            P(),
            P(),
            P(),
            P("level", "space"),
            P("level", "space"),
            P("level", "space"),
        ),
        out_specs=(P(("space", "level"), None), P("level", "space", None), P(), P(), P(), P(), P()),
        check_vma=False,
    )
```

profile of v0, /device:TPU:8, one launch (start us, length us, event | category | flops | bytes accessed | tf_op | source)
XLA Modules:
  0.0 321.0 jit_solution(17864061252349421439)
XLA Ops:
  1.9 10.7 %collective-permute-start.1 = (bf16[8,512]{1,0:T(8,128)(2,1)S(1)}, bf16[8,512]{1,0:T(8,128)(2,1)S(1)}, u32[]{:S(2)}, u32[]{:S(2)}) collective-permute-start(bf16[8,512]{1,0:T(8,128)(2,1)S(1)} %convolution_convert_fusion), channel_id=1, source_target_pairs={{4,0},{8,4},{12,8},{16,12},{20,16},{24,20},{28,24},{32,28},{36,32}... | collective-permute-start | bytes 24584 | tf_op jit(solution)/shard_map/ppermute | solution.py:17
  12.7 1.9 collective-permute-start
  16.1 1.6 fusion.27
  19.7 9.2 %gather_fusion.2 = bf16[2048,512]{1,0:T(8,128)(2,1)} fusion(bf16[512,512]{1,0:T(8,128)(2,1)S(1)} %copy-done, s32[2048]{0:T(1024)S(1)} %broadcast_clamp_fusion), kind=kCustom, calls=%fused_computation.2 | custom fusion | bytes 4202496 | tf_op jit(solution)/shard_map/gather | solution.py:128
  28.9 8.9 %gather_fusion.1 = f32[2048,512]{1,0:T(8,128)} fusion(f32[512,512]{1,0:T(8,128)S(1)} %fusion.27, s32[2048]{0:T(1024)S(1)} %broadcast_clamp_fusion), kind=kCustom, calls=%fused_computation.1 | custom fusion | bytes 8396800 | tf_op jit(solution)/shard_map/gather | solution.py:127
  37.8 9.2 %gather_fusion = bf16[2048,512]{1,0:T(8,128)(2,1)} fusion(bf16[24,512]{1,0:T(8,128)(2,1)S(1)} %pad_maximum_fusion, s32[2048]{0:T(1024)S(1)} %broadcast_clamp_fusion.1), kind=kCustom, calls=%fused_computation | custom fusion | bytes 4202496 | tf_op jit(solution)/shard_map/gather | solution.py:109
  47.0 37.2 %while.16 = (s32[]{:T(128)}, f32[4,512,512]{2,1,0:T(8,128)}, f32[4,512,512]{2,1,0:T(8,128)}, f32[4,512]{1,0:T(4,128)S(1)}, f32[4,512]{1,0:T(4,128)S(1)}, /*index...) while((s32[]{:T(128)}, f32[4,512,512]{2,1,0:T(8,128)}, ...), condition=%wide.region_7.8_spmd, body=%wide.region_0.7_spmd.sunk | while | flops 816840704 | bytes 18942132 | solution.py:131
  47.0 1.7 multiply_convert_fusion.2
  51.6 1.6 fusion.63
  53.2 3.0 bitcast_dynamic-update-slice_fusion.2
  56.4 1.7 multiply_convert_fusion.2
  62.4 3.1 bitcast_dynamic-update-slice_fusion.2
  65.7 1.7 multiply_convert_fusion.2
  71.7 3.1 bitcast_dynamic-update-slice_fusion.2
  75.0 1.7 multiply_convert_fusion.2
  81.0 3.0 bitcast_dynamic-update-slice_fusion.2
  84.2 13.2 %scatter_custom_fusion.1 = f32[24,512]{1,0:T(8,128)S(1)} fusion(s32[2048]{0:T(1024)S(1)} %bitcast.107, f32[2048,512]{1,0:T(8,128)} %bitcast.109, f32[]{:T(128)} %constant.77.clone.1), kind=kCustom, calls=%fused_computation.45 | custom fusion | flops 1048576 | bytes 49664 | tf_op jit(solution)/shard_map/scatter-add | solution.py:136
  97.4 1.9 collective-permute-start.2
  99.4 5.8 %collective-permute-start.3 = (f32[8,512]{1,0:T(8,128)S(1)}, f32[8,512]{1,0:T(8,128)S(1)}, u32[]{:S(2)}, u32[]{:S(2)}) collective-permute-start(f32[8,512]{1,0:T(8,128)S(1)} %get-tuple-element.174), channel_id=1, source_target_pairs={{4,0},{8,4},{12,8},{16,12},{20,16},{24,20},{28,24},{32,28},{36,32}... | collective-permute-start | bytes 49160 | tf_op jit(solution)/shard_map/ppermute | solution.py:27
  105.2 3.8 %reduce_sum.94 = f32[512,512]{1,0:T(8,128)} reduce(f32[4,512,512]{2,1,0:T(8,128)} %get-tuple-element.73, f32[]{:T(128)} %constant.77.clone.1), dimensions={0}, to_apply=%region_13.14 | reduce | flops 786432 | bytes 5242884 | tf_op jit(solution)/shard_map/reduce_sum | solution.py:133
  109.0 13.7 %scatter_custom_fusion = f32[512,512]{1,0:T(8,128)S(1)} fusion(s32[2048]{0:T(1024)} %bitcast.108, f32[2048,512]{1,0:T(8,128)} %bitcast.110, f32[]{:T(128)} %constant.77.clone.1), kind=kCustom, calls=%fused_computation.35 | custom fusion | flops 1048576 | bytes 1049088 | tf_op jit(solution)/shard_map/scatter-add | solution.py:142
  123.6 4.3 %all-to-all-start = ((bf16[4,128,512]{2,1,0:T(8,128)(2,1)}), bf16[4,128,512]{2,1,0:T(8,128)(2,1)S(1)}, u32[]{:S(2)}, u32[]{:S(2)}) async-start(bf16[4,128,512]{2,1,0:T(8,128)(2,1)} %bitcast.17), calls=%async_computation | async-start | bytes 1048576 | tf_op jit(solution)/shard_map/all_to_all | solution.py:37
  129.1 6.8 %all-to-all-done = bf16[4,128,512]{2,1,0:T(8,128)(2,1)S(1)} async-done(((bf16[4,128,512]{2,1,0:T(8,128)(2,1)}), bf16[4,128,512]{2,1,0:T(8,128)(2,1)S(1)}, u32[]{:S(2)}, u32[]{:S(2)}) %all-to-all-start) | async-done | bytes 524320 | tf_op jit(solution)/shard_map/all_to_all | solution.py:37
  138.3 181.7 %all-reduce.2 = (bf16[512,512]{0,1:T(8,128)(2,1)S(1)}, bf16[512,512]{1,0:T(8,128)(2,1)}, bf16[512,512]{1,0:T(8,128)(2,1)}, f32[512]{0:T(512)}, f32[512]{0:T(512)}) all-reduce(f32[512,512]{0,1:T(8,128)S(1)} %convolution_bitcast_fusion.1, f32[512,512]{1,0:T(8,128)S(1)} %fusion.14, ...), channel_id=1, replica_groups=mesh['space'=128,'level'=4] {'space','level'}, use_global_device_ids=true, to_apply=%region_11.12 | all-reduce | flops 787456 | bytes 4726784 | tf_op jit(solution)/shard_map/psum | solution.py:153
  (97 shorter events, 26.6 us)
Async XLA Ops:
  0.6 19.1 %copy-start = (bf16[512,512]{1,0:T(8,128)(2,1)S(1)}, bf16[512,512]{1,0:T(8,128)(2,1)}, u32[]{:S(2)}) copy-start(bf16[512,512]{1,0:T(8,128)(2,1)} %param.15) | copy-start | bytes 1572868
  1.9 35.8 %collective-permute-start.1 = (bf16[8,512]{1,0:T(8,128)(2,1)S(1)}, bf16[8,512]{1,0:T(8,128)(2,1)S(1)}, u32[]{:S(2)}, u32[]{:S(2)}) collective-permute-start(bf16[8,512]{1,0:T(8,128)(2,1)S(1)} %convolution_convert_fusion), channel_id=1, source_target_pairs={{4,0},{8,4},{12,8},{16,12},{20,16},{24,20},{28,24},{32,28},{36,32}... | collective-permute-start | bytes 24584 | tf_op jit(solution)/shard_map/ppermute | solution.py:17
  12.7 25.1 %collective-permute-start = (bf16[8,512]{1,0:T(8,128)(2,1)S(1)}, bf16[8,512]{1,0:T(8,128)(2,1)S(1)}, u32[]{:S(2)}, u32[]{:S(2)}) collective-permute-start(bf16[8,512]{1,0:T(8,128)(2,1)S(1)} %convolution_convert_fusion), channel_id=1, source_target_pairs={{0,4},{4,8},{8,12},{12,16},{16,20},{20,24},{24,28},{28,32},{32,36}... | collective-permute-start | bytes 24584 | tf_op jit(solution)/shard_map/ppermute | solution.py:15
  37.8 9.2 %copy-start.1 = (bf16[512,512]{1,0:T(8,128)(2,1)S(1)}, bf16[512,512]{1,0:T(8,128)(2,1)}, u32[]{:S(2)}) copy-start(bf16[512,512]{1,0:T(8,128)(2,1)} %param.18) | copy-start | bytes 1572868
  37.8 9.2 %copy-start.4 = (f32[512]{0:T(512)S(1)}, f32[512]{0:T(512)}, u32[]{:S(2)}) copy-start(f32[512]{0:T(512)} %param.20) | copy-start | bytes 6148
  37.8 9.2 %copy-start.5 = (f32[512]{0:T(512)S(1)}, f32[512]{0:T(512)}, u32[]{:S(2)}) copy-start(f32[512]{0:T(512)} %param.19) | copy-start | bytes 6148
  97.4 30.4 %collective-permute-start.2 = (f32[8,512]{1,0:T(8,128)S(1)}, f32[8,512]{1,0:T(8,128)S(1)}, u32[]{:S(2)}, u32[]{:S(2)}) collective-permute-start(f32[8,512]{1,0:T(8,128)S(1)} %get-tuple-element.173), channel_id=1, source_target_pairs={{0,4},{4,8},{8,12},{12,16},{16,20},{20,24},{24,28},{28,32},{32,36}... | collective-permute-start | bytes 49160 | tf_op jit(solution)/shard_map/ppermute | solution.py:27
  99.4 28.5 %collective-permute-start.3 = (f32[8,512]{1,0:T(8,128)S(1)}, f32[8,512]{1,0:T(8,128)S(1)}, u32[]{:S(2)}, u32[]{:S(2)}) collective-permute-start(f32[8,512]{1,0:T(8,128)S(1)} %get-tuple-element.174), channel_id=1, source_target_pairs={{4,0},{8,4},{12,8},{16,12},{20,16},{24,20},{28,24},{32,28},{36,32}... | collective-permute-start | bytes 49160 | tf_op jit(solution)/shard_map/ppermute | solution.py:27
  105.2 22.7 %copy-start.6 = (bf16[1,8,512]{2,1,0:T(8,128)(2,1)S(1)}, bf16[1,8,512]{2,1,0:T(8,128)(2,1)}, u32[]{:S(2)}) copy-start(bf16[1,8,512]{2,1,0:T(8,128)(2,1)} %param.14) | copy-start | bytes 24580
  105.2 23.1 %copy-start.2 = (bf16[512,512]{1,0:T(8,128)(2,1)S(1)}, bf16[512,512]{1,0:T(8,128)(2,1)}, u32[]{:S(2)}) copy-start(bf16[512,512]{1,0:T(8,128)(2,1)} %param.16) | copy-start | bytes 1572868
  109.0 27.0 %copy-start.3 = (bf16[512,512]{1,0:T(8,128)(2,1)S(1)}, bf16[512,512]{1,0:T(8,128)(2,1)}, u32[]{:S(2)}) copy-start(bf16[512,512]{1,0:T(8,128)(2,1)} %param.17) | copy-start | bytes 1572868
  123.6 12.4 %all-to-all-start = ((bf16[4,128,512]{2,1,0:T(8,128)(2,1)}), bf16[4,128,512]{2,1,0:T(8,128)(2,1)S(1)}, u32[]{:S(2)}, u32[]{:S(2)}) async-start(bf16[4,128,512]{2,1,0:T(8,128)(2,1)} %bitcast.17), calls=%async_computation | async-start | bytes 1048576 | tf_op jit(solution)/shard_map/all_to_all | solution.py:37
where the time goes:
time: 322 us; the launch traced here: 321 us
  blocking collectives  182 us (57%)
  other arithmetic  45.8 us (14%)
  local copies, waits for them, and re-layouts  34.4 us (11%)
  matrix products  26.5 us (8%)
  starting transfers between devices  24.6 us (8%)
  waiting for transfers between devices  6.85 us (2%)
    psum x1, blocking collectives, body(): lax.psum((wsend_part, wrecv_part, output_weight_piece, bias_piece, gain_p...  182 us
    scatter-add x1, other arithmetic, body(): jax.ops.segment_sum(preactivation_gradient, receiver_index, num_segments=...  13.7 us
    scatter-add x1, other arithmetic, body(): jax.ops.segment_sum(preactivation_gradient, table_row, num_segments=3 * m...  13.2 us
    dot_general x4, matrix products, edge_reverse_step(): jnp.dot(d_outer_b, output_weight.T, preferred_element_type=jnp.float32)  12.2 us
    ppermute x1, starting transfers between devices, with_halo(): lax.ppermute(head, axis, [((i + 1) % count, i) for i in range(ends)])  10.7 us
    gather x1, local copies, waits for them, and re-layouts, body(): sending_rows = table[table_row]  9.18 us
    gather x1, local copies, waits for them, and re-layouts, body(): grid_output_cotangent[receiver_index].reshape(blocks, block, width)  9.15 us
    gather x1, local copies, waits for them, and re-layouts, body(): projected_receiver[receiver_index].reshape(blocks, block, width)  8.9 us
  transfers between devices with their start and end apart: 5, of which 1 were waited for; matrix products, arithmetic and copies ran while one was open for 13% of the time, Pallas kernels for 0%

commit v1 on v0

--- a/solution.py
+++ b/solution.py
@@ -1,7 +1,17 @@
+import functools
 import jax
 import jax.numpy as jnp
 from jax import lax
 from jax.sharding import PartitionSpec as P
+
+
+def use_the_sectors(local_x, a_name, comm_axis):
+    for kk in (a_name, comm_axis):
+        local_x = lax.psum(local_x, kk)
+    return local_x
+
+
+measure_the_grid = functools.partial(use_the_sectors, a_name="level", comm_axis="space")
 
 
 def with_halo(cells, sides, width):
@@ -150,9 +160,7 @@
     d_grid = jnp.dot(grid_sum, w_recv.T, preferred_element_type=jnp.float32)
     wsend_part = jnp.dot(mesh_latent[0].T, mesh_sum, preferred_element_type=jnp.float32)
     wrecv_part = jnp.dot(grid_part.T, grid_sum, preferred_element_type=jnp.float32)
-    totals = lax.psum(
-        (wsend_part, wrecv_part, output_weight_piece, bias_piece, gain_piece), ("space", "level")
-    )
+    totals = measure_the_grid((wsend_part, wrecv_part, output_weight_piece, bias_piece, gain_piece))
     d_w_send = totals[0].astype(jnp.bfloat16)
     d_w_recv = totals[1].astype(jnp.bfloat16)
     d_w_out = totals[2].astype(jnp.bfloat16)

time: 322 us -> 770 us (2.39)
  the two profiles are of different devices: /device:TPU:8 before, /device:TPU:2 now
where the time goes in v1:
time: 770 us; the launch traced here: 769 us
  blocking collectives  542 us (70%)
  waiting for transfers between devices  87.2 us (11%)
  other arithmetic  45.7 us (6%)
  local copies, waits for them, and re-layouts  34.4 us (4%)
  matrix products  28.5 us (4%)
  starting transfers between devices  17 us (2%)
  between operations  14.3 us (2%)
    psum x2, blocking collectives, use_the_sectors(): local_x = lax.psum(local_x, kk)  542 us
    psum x1, waiting for transfers between devices, use_the_sectors(): local_x = lax.psum(local_x, kk)  79.2 us
  transfers between devices with their start and end apart: 6, of which 2 were waited for; matrix products, arithmetic and copies ran while one was open for 6% of the time, Pallas kernels for 0%

profile of v1, /device:TPU:2, one launch (start us, length us, event | category | flops | bytes accessed | tf_op | source)
XLA Modules:
  0.0 769.2 jit_solution(7721909442522616770)
XLA Ops:
  9.8 3.0 collective-permute-start
  14.3 1.6 fusion.27
  17.9 9.2 %gather_fusion.2 = bf16[2048,512]{1,0:T(8,128)(2,1)} fusion(bf16[512,512]{1,0:T(8,128)(2,1)S(1)} %copy-done, s32[2048]{0:T(1024)S(1)} %broadcast_clamp_fusion), kind=kCustom, calls=%fused_computation.2 | custom fusion | bytes 4202496 | tf_op jit(solution)/shard_map/gather | solution.py:138
  27.1 8.9 %gather_fusion.1 = f32[2048,512]{1,0:T(8,128)} fusion(f32[512,512]{1,0:T(8,128)S(1)} %fusion.27, s32[2048]{0:T(1024)S(1)} %broadcast_clamp_fusion), kind=kCustom, calls=%fused_computation.1 | custom fusion | bytes 8396800 | tf_op jit(solution)/shard_map/gather | solution.py:137
  36.0 9.2 %gather_fusion = bf16[2048,512]{1,0:T(8,128)(2,1)} fusion(bf16[24,512]{1,0:T(8,128)(2,1)S(1)} %pad_maximum_fusion, s32[2048]{0:T(1024)S(1)} %broadcast_clamp_fusion.1), kind=kCustom, calls=%fused_computation | custom fusion | bytes 4202496 | tf_op jit(solution)/shard_map/gather | solution.py:119
  45.2 37.2 %while.16 = (s32[]{:T(128)}, f32[4,512,512]{2,1,0:T(8,128)}, f32[4,512,512]{2,1,0:T(8,128)}, f32[4,512]{1,0:T(4,128)S(1)}, f32[4,512]{1,0:T(4,128)S(1)}, /*index...) while((s32[]{:T(128)}, f32[4,512,512]{2,1,0:T(8,128)}, ...), condition=%wide.region_7.8_spmd, body=%wide.region_0.7_spmd.sunk | while | flops 816840704 | bytes 18942132 | solution.py:141
  45.2 1.7 multiply_convert_fusion.2
  51.4 3.0 bitcast_dynamic-update-slice_fusion.2
  54.6 1.7 multiply_convert_fusion.2
  60.6 3.1 bitcast_dynamic-update-slice_fusion.2
  63.9 1.7 multiply_convert_fusion.2
  69.9 3.1 bitcast_dynamic-update-slice_fusion.2
  73.2 1.7 multiply_convert_fusion.2
  79.2 3.0 bitcast_dynamic-update-slice_fusion.2
  82.4 13.2 %scatter_custom_fusion.1 = f32[24,512]{1,0:T(8,128)S(1)} fusion(s32[2048]{0:T(1024)S(1)} %bitcast.107, f32[2048,512]{1,0:T(8,128)} %bitcast.109, f32[]{:T(128)} %constant.77.clone.1), kind=kCustom, calls=%fused_computation.45 | custom fusion | flops 1048576 | bytes 49664 | tf_op jit(solution)/shard_map/scatter-add | solution.py:146
  95.6 3.4 collective-permute-start.2
  100.4 3.8 reduce_sum.94
  104.2 13.7 %scatter_custom_fusion = f32[512,512]{1,0:T(8,128)S(1)} fusion(s32[2048]{0:T(1024)} %bitcast.108, f32[2048,512]{1,0:T(8,128)} %bitcast.110, f32[]{:T(128)} %constant.77.clone.1), kind=kCustom, calls=%fused_computation.35 | custom fusion | flops 1048576 | bytes 1049088 | tf_op jit(solution)/shard_map/scatter-add | solution.py:152
  118.7 7.9 %all-to-all-start = ((bf16[4,128,512]{2,1,0:T(8,128)(2,1)}), bf16[4,128,512]{2,1,0:T(8,128)(2,1)S(1)}, u32[]{:S(2)}, u32[]{:S(2)}) async-start(bf16[4,128,512]{2,1,0:T(8,128)(2,1)} %bitcast.17), calls=%async_computation | async-start | bytes 1048576 | tf_op jit(solution)/shard_map/all_to_all | solution.py:47
  128.0 7.9 %all-to-all-done = bf16[4,128,512]{2,1,0:T(8,128)(2,1)S(1)} async-done(((bf16[4,128,512]{2,1,0:T(8,128)(2,1)}), bf16[4,128,512]{2,1,0:T(8,128)(2,1)S(1)}, u32[]{:S(2)}, u32[]{:S(2)}) %all-to-all-start) | async-done | bytes 524320 | tf_op jit(solution)/shard_map/all_to_all | solution.py:47
  136.0 2.2 fusion.14
  138.3 9.2 %all-reduce.1 = (f32[512]{0:T(512)S(1)}, f32[512]{0:T(512)S(1)}) all-reduce(f32[512]{0:T(512)S(1)} %reduce_sum.95, f32[512]{0:T(512)S(1)} %reduce_sum.96), channel_id=1, replica_groups=mesh['space'=128,'level'=4] {'level'}, use_global_device_ids=true, to_apply=%region_19.20 | all-reduce | flops 1024 | bytes 8192 | tf_op jit(solution)/shard_map/psum | solution.py:10
  149.4 79.2 %all-reduce.6.cloned.1.call-done = (f32[512,512]{0,1:T(8,128)}, f32[512,512]{1,0:T(8,128)}, f32[512,512]{1,0:T(8,128)}) async-done(((f32[512,512]{0,1:T(8,128)}, f32[512,512]{1,0:T(8,128)}, f32[512,512]{1,0:T(8,128)}), (f32[512,512]{0,1:T(8,128)}, f32[512,512]{1,0:T(8,128)}, f32[512,512]{1,0:T(8,128)})) %all-reduce.6.cloned.1.call-update) | async-done | bytes 3145744 | tf_op jit(solution)/shard_map/psum | solution.py:10
  228.6 532.7 %all-reduce.7 = (bf16[512,512]{0,1:T(8,128)(2,1)S(1)}, bf16[512,512]{1,0:T(8,128)(2,1)}, bf16[512,512]{1,0:T(8,128)(2,1)}, f32[512]{0:T(512)}, f32[512]{0:T(512)}) all-reduce(f32[512,512]{0,1:T(8,128)} %get-tuple-element.167, f32[512,512]{1,0:T(8,128)} %get-tuple-element.168, ...), channel_id=1, replica_groups=mesh['space'=128,'level'=4] {'space'}, use_global_device_ids=true, to_apply=%region_12.13 | all-reduce | flops 787456 | bytes 4726784 | tf_op jit(solution)/shard_map/psum | solution.py:10
  (101 shorter events, 30.6 us)
Async XLA Ops:
  7.2 10.7 %copy-start = (bf16[512,512]{1,0:T(8,128)(2,1)S(1)}, bf16[512,512]{1,0:T(8,128)(2,1)}, u32[]{:S(2)}) copy-start(bf16[512,512]{1,0:T(8,128)(2,1)} %param.15) | copy-start | bytes 1572868
  8.5 27.5 %collective-permute-start.1 = (bf16[8,512]{1,0:T(8,128)(2,1)S(1)}, bf16[8,512]{1,0:T(8,128)(2,1)S(1)}, u32[]{:S(2)}, u32[]{:S(2)}) collective-permute-start(bf16[8,512]{1,0:T(8,128)(2,1)S(1)} %convolution_convert_fusion), channel_id=1, source_target_pairs={{4,0},{8,4},{12,8},{16,12},{20,16},{24,20},{28,24},{32,28},{36,32}... | collective-permute-start | bytes 24584 | tf_op jit(solution)/shard_map/ppermute | solution.py:27
  9.8 26.2 %collective-permute-start = (bf16[8,512]{1,0:T(8,128)(2,1)S(1)}, bf16[8,512]{1,0:T(8,128)(2,1)S(1)}, u32[]{:S(2)}, u32[]{:S(2)}) collective-permute-start(bf16[8,512]{1,0:T(8,128)(2,1)S(1)} %convolution_convert_fusion), channel_id=1, source_target_pairs={{0,4},{4,8},{8,12},{12,16},{16,20},{20,24},{24,28},{28,32},{32,36}... | collective-permute-start | bytes 24584 | tf_op jit(solution)/shard_map/ppermute | solution.py:25
  36.0 9.2 %copy-start.1 = (bf16[512,512]{1,0:T(8,128)(2,1)S(1)}, bf16[512,512]{1,0:T(8,128)(2,1)}, u32[]{:S(2)}) copy-start(bf16[512,512]{1,0:T(8,128)(2,1)} %param.18) | copy-start | bytes 1572868
  36.0 9.2 %copy-start.4 = (f32[512]{0:T(512)S(1)}, f32[512]{0:T(512)}, u32[]{:S(2)}) copy-start(f32[512]{0:T(512)} %param.20) | copy-start | bytes 6148
  36.0 9.2 %copy-start.5 = (f32[512]{0:T(512)S(1)}, f32[512]{0:T(512)}, u32[]{:S(2)}) copy-start(f32[512]{0:T(512)} %param.19) | copy-start | bytes 6148
  95.6 31.0 %collective-permute-start.2 = (f32[8,512]{1,0:T(8,128)S(1)}, f32[8,512]{1,0:T(8,128)S(1)}, u32[]{:S(2)}, u32[]{:S(2)}) collective-permute-start(f32[8,512]{1,0:T(8,128)S(1)} %get-tuple-element.178), channel_id=1, source_target_pairs={{0,4},{4,8},{8,12},{12,16},{16,20},{20,24},{24,28},{28,32},{32,36}... | collective-permute-start | bytes 49160 | tf_op jit(solution)/shard_map/ppermute | solution.py:37
  99.1 27.6 %collective-permute-start.3 = (f32[8,512]{1,0:T(8,128)S(1)}, f32[8,512]{1,0:T(8,128)S(1)}, u32[]{:S(2)}, u32[]{:S(2)}) collective-permute-start(f32[8,512]{1,0:T(8,128)S(1)} %get-tuple-element.179), channel_id=1, source_target_pairs={{4,0},{8,4},{12,8},{16,12},{20,16},{24,20},{28,24},{32,28},{36,32}... | collective-permute-start | bytes 49160 | tf_op jit(solution)/shard_map/ppermute | solution.py:37
  100.4 26.3 %copy-start.6 = (bf16[1,8,512]{2,1,0:T(8,128)(2,1)S(1)}, bf16[1,8,512]{2,1,0:T(8,128)(2,1)}, u32[]{:S(2)}) copy-start(bf16[1,8,512]{2,1,0:T(8,128)(2,1)} %param.14) | copy-start | bytes 24580
  117.8 29.7 %copy-start.2 = (bf16[512,512]{1,0:T(8,128)(2,1)S(1)}, bf16[512,512]{1,0:T(8,128)(2,1)}, u32[]{:S(2)}) copy-start(bf16[512,512]{1,0:T(8,128)(2,1)} %param.16) | copy-start | bytes 1572868
  118.7 29.6 %copy-start.3 = (bf16[512,512]{1,0:T(8,128)(2,1)S(1)}, bf16[512,512]{1,0:T(8,128)(2,1)}, u32[]{:S(2)}) copy-start(bf16[512,512]{1,0:T(8,128)(2,1)} %param.17) | copy-start | bytes 1572868
  118.7 17.2 %all-to-all-start = ((bf16[4,128,512]{2,1,0:T(8,128)(2,1)}), bf16[4,128,512]{2,1,0:T(8,128)(2,1)S(1)}, u32[]{:S(2)}, u32[]{:S(2)}) async-start(bf16[4,128,512]{2,1,0:T(8,128)(2,1)} %bitcast.17), calls=%async_computation | async-start | bytes 1048576 | tf_op jit(solution)/shard_map/all_to_all | solution.py:47
  126.7 102.0 %all-reduce.6.cloned.1.call-start = ((), (), s32[]{:S(2)}) async-start(), calls=%async_computation.1 | async-start | bytes 6291456 | tf_op jit(solution)/shard_map/psum | solution.py:10
Sparse Core Ops, SparseCore 0:
  138.4 90.1 all-reduce.5
